TPU v7x, 32 devices: a whole 2x2x4 slice. The times are simulated.
32 devices in a mesh: depth: 2 (over x), row: 4 (over y, core), col: 4 (over z).
Axes of the slice: x: 2, y: 2, z: 4, core: 2. Of those that a mesh axis runs over, the one named last changes fastest.
Arguments:
- q_slab: float32 [1536, 1024], P('col', ('depth', 'row')), may hold values from -6 to 6
- triangle: float32 [1024, 1024], P(None, 'depth'), as said below
- panel_q: float32 [32768, 1024], P('row', ('depth', 'col')), may hold values from -0.1875 to 0.1875
Outputs:
- slab_out: float32 [1536, 32768], P('col', 'row')
Inputs may be any that keep to these rules, and one draw needn't show every extreme that they name: triangle is zero below its diagonal; its diagonal lies in 0.5 to 1.5.
All inputs are finite; a program needn't handle non-finite values.
Results may differ from a plain program's by a relative error of at most 0.000071.
Values sent between devices are 32-bit elements; how exact they have to be, the bound alone decides.
A program may use at most 64 MiB of HBM per device.

v0:
```python
import jax
import jax.numpy as jnp
from jax import lax
from jax.sharding import PartitionSpec as P


def per_device(q_slab, triangle, panel_q):
    rows = q_slab.shape[0]
    width = triangle.shape[1]
    share = width // lax.axis_size("row")
    factor = lax.dynamic_slice_in_dim(triangle, lax.axis_index("row") * share, share, 1)
    left = jnp.dot(
        lax.all_gather(q_slab, ("depth", "row"), axis=1, tiled=True),
        factor,
        precision=lax.Precision.HIGHEST,
        preferred_element_type=jnp.float32,
    )
    left = lax.all_gather(left, "row", axis=1, tiled=True)
    narrow = panel_q.shape[1]
    columns = lax.axis_size("col")
    mixed = lax.all_to_all(panel_q, "depth", split_axis=0, concat_axis=1, tiled=True)
    left_all = lax.all_gather(left, "depth", axis=1, tiled=True)
    grid = left_all.reshape(rows, 2, columns, narrow)
    piece = lax.all_gather(mixed, "col", axis=1, tiled=True)
    count = piece.shape[1] // (2 * narrow)
    pieces = piece.reshape(piece.shape[0], count, 2, narrow)
    partial_out = jnp.einsum(
        "sdnw,rndw->sr",
        grid,
        pieces,
        precision=lax.Precision.HIGHEST,
        preferred_element_type=jnp.float32,
    )
    return lax.all_gather(partial_out, "depth", axis=1, tiled=True)


def solution(mesh):
    placed = (P("col", ("depth", "row")), P(None, "depth"), P("row", ("depth", "col")))
    return jax.shard_map(
        per_device, mesh=mesh, in_specs=placed, out_specs=P("col", "row"), check_vma=False
    )
```

profile of v0, /device:TPU:0, one launch (start us, length us, event | category | flops | bytes accessed | tf_op | source)
XLA Modules:
  0.0 567.0 jit_solution(8736152346896375355)
XLA Ops:
  6.5 0.0 copy-start
  6.5 0.0 all-gather.5.cloned.1.call-start
  6.5 0.7 all-gather.5.cloned.1.call-update
  7.3 5.6 all-to-all-start
  12.9 0.0 all-gather.7.cloned.1.call-start
  12.9 31.0 %all-gather.5.cloned.1.call-done = f32[384,1024]{1,0:T(8,128)} async-done(((f32[384,128]{1,0:T(8,128)}), f32[384,1024]{1,0:T(8,128)}) %all-gather.5.cloned.1.call-update) | async-done | bytes 1572880 | tf_op jit(solution)/shard_map/all_gather | solution.py:13
  44.0 0.0 copy-done
  44.0 3.3 convolution_bitcast_fusion
  47.3 9.1 %all_gather.16 = f32[384,512]{0,1:T(8,128)} all-gather(f32[384,128]{0,1:T(8,128)S(1)} %convolution_bitcast_fusion), channel_id=1, replica_groups=mesh['depth'=2,'row'=4,'col'=4] {'row'}, dimensions={1}, use_global_device_ids=true | all-gather | bytes 983040 | tf_op jit(solution)/shard_map/all_gather | solution.py:18
  56.4 0.0 all-gather.7.cloned.1.call-update
  56.4 0.0 all-gather.9.cloned.1.call-start
  56.5 13.7 %all-to-all-done = f32[2,4096,128]{2,1,0:T(8,128)} async-done(((f32[2,4096,128]{2,1,0:T(8,128)}), f32[2,4096,128]{2,1,0:T(8,128)}, u32[]{:S(2)}, u32[]{:S(2)}) %all-to-all-start) | async-done | bytes 4194336 | tf_op jit(solution)/shard_map/all_to_all | solution.py:21
  70.2 5.6 copy.7
  75.8 0.0 all-gather.9.cloned.1.call-update
  75.8 0.0 all-gather.11.cloned.1.call-start
  75.8 9.2 %all-gather.7.cloned.1.call-done = f32[384,1024]{0,1:T(8,128)} async-done(((f32[384,512]{0,1:T(8,128)}), f32[384,1024]{0,1:T(8,128)}) %all-gather.7.cloned.1.call-update) | async-done | bytes 1572880 | tf_op jit(solution)/shard_map/all_gather | solution.py:22
  85.1 288.9 %all-gather.9.cloned.1.call-done = f32[4096,1024]{0,1:T(8,128)} async-done(((f32[4096,256]{0,1:T(8,128)}), f32[4096,1024]{0,1:T(8,128)}) %all-gather.9.cloned.1.call-update) | async-done | bytes 16777232 | tf_op jit(solution)/shard_map/all_gather | solution.py:24
  374.0 24.7 %fusion.2 = f32[384,4096]{1,0:T(8,128)} fusion(f32[384,2,4,128]{0,3,2,1:T(8,128)} %bitcast.16, f32[4096,4,2,128]{0,3,2,1:T(8,128)} %bitcast.13), kind=kOutput, calls=%fused_computation.2 | convolution fusion | flops 19327352832 | bytes 24641536 | tf_op jit(solution)/shard_map/sdnw,rndw->sr/dot_general | solution.py:27
  398.7 0.0 all-gather.11.cloned.1.call-update
  398.7 150.8 %all-gather.11.cloned.1.call-done = f32[384,8192]{1,0:T(8,128)} async-done(((f32[384,4096]{1,0:T(8,128)}), f32[384,8192]{1,0:T(8,128)}) %all-gather.11.cloned.1.call-update) | async-done | bytes 12582928 | tf_op jit(solution)/shard_map/all_gather | solution.py:34
  549.6 0.0 copy-start.1
  549.6 10.9 %copy.19 = f32[384,8192]{1,0:T(8,128)} copy(f32[384,8192]{1,0:T(8,128)} %all-gather.11.cloned.1.call-done) | data formatting | bytes 25165824
  560.5 0.0 copy-done.1
Async XLA Ops:
  6.5 37.4 %copy-start = (f32[1024,512]{1,0:T(8,128)S(1)}, f32[1024,512]{1,0:T(8,128)}, u32[]{:S(2)}) copy-start(f32[1024,512]{1,0:T(8,128)} %param.4) | copy-start | bytes 6291460
  6.5 37.4 %all-gather.5.cloned.1.call-start = ((), (), s32[]{:S(2)}) async-start(), calls=%async_computation.1 | async-start | bytes 1769472 | tf_op jit(solution)/shard_map/all_gather | solution.py:13
  7.3 62.9 %all-to-all-start = ((f32[2,4096,128]{2,1,0:T(8,128)}), f32[2,4096,128]{2,1,0:T(8,128)}, u32[]{:S(2)}, u32[]{:S(2)}) async-start(f32[2,4096,128]{2,1,0:T(8,128)} %bitcast.15), calls=%async_computation | async-start | bytes 8388608 | tf_op jit(solution)/shard_map/all_to_all | solution.py:21
  12.9 72.2 %all-gather.7.cloned.1.call-start = ((), (), s32[]{:S(2)}) async-start(), calls=%async_computation.2 | async-start | bytes 2359296 | tf_op jit(solution)/shard_map/all_gather | solution.py:22
  56.4 317.6 %all-gather.9.cloned.1.call-start = ((), (), s32[]{:S(2)}) async-start(), calls=%async_computation.3 | async-start | bytes 20971520 | tf_op jit(solution)/shard_map/all_gather | solution.py:24
  75.8 473.8 %all-gather.11.cloned.1.call-start = ((), (), s32[]{:S(2)}) async-start(), calls=%async_computation.4 | async-start | bytes 18874368 | tf_op jit(solution)/shard_map/all_gather | solution.py:34
  549.6 10.9 %copy-start.1 = (f32[1024,512]{1,0:T(8,128)S(1)}, f32[1024,512]{1,0:T(8,128)}, u32[]{:S(2)}) copy-start(f32[1024,512]{1,0:T(8,128)} %param.4) | copy-start | bytes 6291460
Sparse Core Ops, SparseCore 0:
  9.2 34.7 all-gather.4
  56.6 28.4 all-gather.6
  86.6 287.3 all-gather.8
  398.8 150.6 all-gather.10
where the time goes:
time: 567 us
  waiting for transfers between devices  494 us (87%)
  matrix products  28 us (5%)
  local copies, waits for them, and re-layouts  16.5 us (3%)
  between operations  13.1 us (2%)
  blocking collectives  9.12 us (2%)
  starting transfers between devices  5.74 us (1%)
    all_gather x1, waiting for transfers between devices, per_device(): piece = lax.all_gather(mixed, 'col', axis=1, tiled=True)  289 us
    all_gather x1, waiting for transfers between devices, per_device(): return lax.all_gather(partial_out, 'depth', axis=1, tiled=True)  151 us
    all_gather x1, waiting for transfers between devices, per_device(): lax.all_gather(q_slab, ('depth', 'row'), axis=1, tiled=True)  31 us
    dot_general x1, matrix products, per_device(): jnp.einsum('sdnw,rndw->sr', grid, pieces, precision=lax.Precision.HIGHEST...  24.7 us
    all_to_all x1, waiting for transfers between devices, per_device(): lax.all_to_all(panel_q, 'depth', split_axis=0, concat_axis=1, tiled=True)  13.7 us
  transfers between devices with their start and end apart: 5, of which 5 were waited for; matrix products, arithmetic and copies ran while one was open for 2% of the time, Pallas kernels for 0%

commit v1 on v0

--- a/solution.py
+++ b/solution.py
@@ -2,6 +2,12 @@
 import jax.numpy as jnp
 from jax import lax
 from jax.sharding import PartitionSpec as P
+
+
+def stack_and_merge(shard, axis, dim):
+    shards = lax.all_gather(shard, axis, axis=0, tiled=False)
+    whole = jnp.concatenate(shards, axis=dim)
+    return whole
 
 
 def per_device(q_slab, triangle, panel_q):
@@ -31,7 +37,7 @@
         precision=lax.Precision.HIGHEST,
         preferred_element_type=jnp.float32,
     )
-    return lax.all_gather(partial_out, "depth", axis=1, tiled=True)
+    return stack_and_merge(partial_out, "depth", 1)
 
 
 def solution(mesh):

time: 567 us -> 567 us (level)
    reshape x0 -> x1, local copies, waits for them, and re-layouts: none -> 11.1 us  [stack_and_merge(): whole = jnp.concatenate(shards, axis=dim)]
    unnamed x5 -> x4, local copies, waits for them, and re-layouts: 10.9 us -> 0.01 us
where the time goes in v1:
time: 567 us
  waiting for transfers between devices  494 us (87%)
  matrix products  28 us (5%)
  local copies, waits for them, and re-layouts  16.7 us (3%)
  between operations  13.1 us (2%)
  blocking collectives  9.12 us (2%)
  starting transfers between devices  5.74 us (1%)
    all_gather x1, waiting for transfers between devices, per_device(): piece = lax.all_gather(mixed, 'col', axis=1, tiled=True)  289 us
    all_gather x1, waiting for transfers between devices, stack_and_merge(): shards = lax.all_gather(shard, axis, axis=0, tiled=False)  151 us
    all_gather x1, waiting for transfers between devices, per_device(): lax.all_gather(q_slab, ('depth', 'row'), axis=1, tiled=True)  31 us
    dot_general x1, matrix products, per_device(): jnp.einsum('sdnw,rndw->sr', grid, pieces, precision=lax.Precision.HIGHEST...  24.7 us
    all_to_all x1, waiting for transfers between devices, per_device(): lax.all_to_all(panel_q, 'depth', split_axis=0, concat_axis=1, tiled=True)  13.7 us
  transfers between devices with their start and end apart: 5, of which 5 were waited for; matrix products, arithmetic and copies ran while one was open for 2% of the time, Pallas kernels for 0%

profile of v1, /device:TPU:0, one launch (start us, length us, event | category | flops | bytes accessed | tf_op | source)
XLA Modules:
  0.0 567.2 jit_solution(2484230032205384579)
XLA Ops:
  6.5 0.0 copy-start
  6.5 0.0 all-gather.6.cloned.1.call-start
  6.5 0.7 all-gather.6.cloned.1.call-update
  7.3 5.6 all-to-all-start
  12.9 0.0 all-gather.8.cloned.1.call-start
  12.9 31.0 %all-gather.6.cloned.1.call-done = f32[384,1024]{1,0:T(8,128)} async-done(((f32[384,128]{1,0:T(8,128)}), f32[384,1024]{1,0:T(8,128)}) %all-gather.6.cloned.1.call-update) | async-done | bytes 1572880 | tf_op jit(solution)/shard_map/all_gather | solution.py:19
  44.0 0.0 copy-done
  44.0 3.3 convolution_bitcast_fusion
  47.3 9.1 %all_gather.19 = f32[384,512]{0,1:T(8,128)} all-gather(f32[384,128]{0,1:T(8,128)S(1)} %convolution_bitcast_fusion), channel_id=1, replica_groups=mesh['depth'=2,'row'=4,'col'=4] {'row'}, dimensions={1}, use_global_device_ids=true | all-gather | bytes 983040 | tf_op jit(solution)/shard_map/all_gather | solution.py:24
  56.4 0.0 all-gather.8.cloned.1.call-update
  56.4 0.0 all-gather.10.cloned.1.call-start
  56.5 13.7 %all-to-all-done = f32[2,4096,128]{2,1,0:T(8,128)} async-done(((f32[2,4096,128]{2,1,0:T(8,128)}), f32[2,4096,128]{2,1,0:T(8,128)}, u32[]{:S(2)}, u32[]{:S(2)}) %all-to-all-start) | async-done | bytes 4194336 | tf_op jit(solution)/shard_map/all_to_all | solution.py:27
  70.2 5.6 copy.9
  75.8 0.0 all-gather.10.cloned.1.call-update
  75.8 0.0 all-gather.12.cloned.1.call-start
  75.8 9.2 %all-gather.8.cloned.1.call-done = f32[384,1024]{0,1:T(8,128)} async-done(((f32[384,512]{0,1:T(8,128)}), f32[384,1024]{0,1:T(8,128)}) %all-gather.8.cloned.1.call-update) | async-done | bytes 1572880 | tf_op jit(solution)/shard_map/all_gather | solution.py:28
  85.1 288.9 %all-gather.10.cloned.1.call-done = f32[4096,1024]{0,1:T(8,128)} async-done(((f32[4096,256]{0,1:T(8,128)}), f32[4096,1024]{0,1:T(8,128)}) %all-gather.10.cloned.1.call-update) | async-done | bytes 16777232 | tf_op jit(solution)/shard_map/all_gather | solution.py:30
  374.0 24.7 %fusion.2 = f32[384,4096]{1,0:T(8,128)} fusion(f32[384,2,4,128]{0,3,2,1:T(8,128)} %bitcast.22, f32[4096,4,2,128]{0,3,2,1:T(8,128)} %bitcast.18), kind=kOutput, calls=%fused_computation.2 | convolution fusion | flops 19327352832 | bytes 24641536 | tf_op jit(solution)/shard_map/sdnw,rndw->sr/dot_general | solution.py:33
  398.7 0.0 all-gather.12.cloned.1.call-update
  398.7 150.8 %all-gather.12.cloned.1.call-done = f32[768,4096]{1,0:T(8,128)} async-done(((f32[384,4096]{1,0:T(8,128)}), f32[768,4096]{1,0:T(8,128)}) %all-gather.12.cloned.1.call-update) | async-done | bytes 12582928 | tf_op jit(solution)/shard_map/all_gather | solution.py:8
  549.6 0.0 copy-start.1
  549.6 11.1 %copy.17 = f32[2,48,8,4096]{3,2,0,1:T(8,128)} copy(f32[2,48,8,4096]{3,2,1,0:T(8,128)} %bitcast.20) | data formatting | bytes 25165824 | tf_op jit(solution)/shard_map/reshape | solution.py:9
  560.6 0.0 copy-done.1
Async XLA Ops:
  6.5 37.4 %copy-start = (f32[1024,512]{1,0:T(8,128)S(1)}, f32[1024,512]{1,0:T(8,128)}, u32[]{:S(2)}) copy-start(f32[1024,512]{1,0:T(8,128)} %param.4) | copy-start | bytes 6291460
  6.5 37.4 %all-gather.6.cloned.1.call-start = ((), (), s32[]{:S(2)}) async-start(), calls=%async_computation.1 | async-start | bytes 1769472 | tf_op jit(solution)/shard_map/all_gather | solution.py:19
  7.3 62.9 %all-to-all-start = ((f32[2,4096,128]{2,1,0:T(8,128)}), f32[2,4096,128]{2,1,0:T(8,128)}, u32[]{:S(2)}, u32[]{:S(2)}) async-start(f32[2,4096,128]{2,1,0:T(8,128)} %bitcast.21), calls=%async_computation | async-start | bytes 8388608 | tf_op jit(solution)/shard_map/all_to_all | solution.py:27
  12.9 72.2 %all-gather.8.cloned.1.call-start = ((), (), s32[]{:S(2)}) async-start(), calls=%async_computation.2 | async-start | bytes 2359296 | tf_op jit(solution)/shard_map/all_gather | solution.py:28
  56.4 317.6 %all-gather.10.cloned.1.call-start = ((), (), s32[]{:S(2)}) async-start(), calls=%async_computation.3 | async-start | bytes 20971520 | tf_op jit(solution)/shard_map/all_gather | solution.py:30
  75.8 473.8 %all-gather.12.cloned.1.call-start = ((), (), s32[]{:S(2)}) async-start(), calls=%async_computation.4 | async-start | bytes 18874368 | tf_op jit(solution)/shard_map/all_gather | solution.py:8
  549.6 11.1 %copy-start.1 = (f32[1024,512]{1,0:T(8,128)S(1)}, f32[1024,512]{1,0:T(8,128)}, u32[]{:S(2)}) copy-start(f32[1024,512]{1,0:T(8,128)} %param.4) | copy-start | bytes 6291460
Sparse Core Ops, SparseCore 0:
  9.2 34.7 all-gather.5
  56.6 28.4 all-gather.7
  86.6 287.3 all-gather.9
  398.8 150.6 all-gather.11
